TPU v7x, 32 devices: a whole 2x2x4 slice. The times are simulated.
32 devices in a mesh: lat: 8 (over z, y), lon: 4 (over x, core).
Axes of the slice: x: 2, y: 2, z: 4, core: 2. Of those that a mesh axis runs over, the one named last changes fastest.
Arguments:
- predicted_state: bfloat16 [222, 320, 512], P(None, 'lat', 'lon'), may hold values from -30 to 30
- observed_state: bfloat16 [222, 320, 512], P(None, 'lat', 'lon'), may hold values from -30 to 30
- longterm_average_state: bfloat16 [222, 320, 512], P(None, 'lat', 'lon'), may hold values from -30 to 30
Outputs:
- blurred_mismatch_map: bfloat16 [222, 320, 512], P(None, 'lat', 'lon')
- quadratic_mean_mistake: float32 [222], replicated
- pattern_agreement: float32 [222], replicated
All inputs are finite; a program needn't handle non-finite values.
Results may differ from a plain program's by a relative error of at most 0.00155.
Values may be sent and summed in bfloat16 or wider, within the bound.
A program may use at most 128 MiB of HBM per device.

v0:
```python
import jax
import jax.numpy as jnp
from jax import lax
from jax.sharding import PartitionSpec as P

epsilon = 1e-06


def extended(cells, sides, width):
    for axis, dim in sides:
        count = lax.axis_size(axis)
        head = lax.slice_in_dim(cells, 0, width, axis=dim)
        tail = lax.slice_in_dim(cells, cells.shape[dim] - width, cells.shape[dim], axis=dim)
        cells = jnp.concatenate(
            [
                lax.ppermute(tail, axis, [(i, (i + 1) % count) for i in range(count)]),
                cells,
                lax.ppermute(head, axis, [((i + 1) % count, i) for i in range(count)]),
            ],
            axis=dim,
        )
    return cells


def deviation_from_normal(predicted_state, observed_state, longterm_average_state):
    normal_reference_state = longterm_average_state.astype(jnp.float32)
    return (
        predicted_state.astype(jnp.float32) - normal_reference_state,
        observed_state.astype(jnp.float32) - normal_reference_state,
    )


def vertical_sum(member):
    return member[:, :-2] + member[:, 1:-1] + member[:, 2:]


def horizontal_sum(member):
    return member[:, :, :-2] + member[:, :, 1:-1] + member[:, :, 2:]


def finish(running_accumulations, grid_cells):
    mean_fcst = running_accumulations[1] / grid_cells
    mean_true = running_accumulations[2] / grid_cells
    variance_fcst = running_accumulations[3] / grid_cells - mean_fcst * mean_fcst
    variance_true = running_accumulations[4] / grid_cells - mean_true * mean_true
    covariance = running_accumulations[5] / grid_cells - mean_fcst * mean_true
    quadratic_mean_mistake = jnp.sqrt(running_accumulations[0] / grid_cells)
    pattern_agreement = covariance / jnp.sqrt((variance_fcst + epsilon) * (variance_true + epsilon))
    return (quadratic_mean_mistake, pattern_agreement)


def local(predicted_state, observed_state, longterm_average_state):
    nearby_parallel_accumulated = predicted_state.shape[1]
    parallel_overall_accumulated = nearby_parallel_accumulated * lax.axis_size("lat")
    meridian_accumulated = predicted_state.shape[2] * lax.axis_size("lon")
    row_start = lax.axis_index("lat") * nearby_parallel_accumulated
    row_index = row_start + jnp.arange(nearby_parallel_accumulated, dtype=jnp.int32)
    stacked_inputs = jnp.stack([predicted_state, observed_state, longterm_average_state])
    rimmed = extended(stacked_inputs, (("lat", 2), ("lon", 3)), 1)
    widened = deviation_from_normal(rimmed[0], rimmed[1], rimmed[2])
    padded_index = row_start - 1 + jnp.arange(nearby_parallel_accumulated + 2, dtype=jnp.int32)
    inside = ((padded_index >= 0) & (padded_index < parallel_overall_accumulated)).astype(
        jnp.float32
    )[None, :, None]
    summed = tuple((horizontal_sum(vertical_sum(member * inside)) for member in widened))
    row_count = (
        3.0
        - (row_index == 0).astype(jnp.float32)
        - (row_index == parallel_overall_accumulated - 1).astype(jnp.float32)
    )
    divisor = (3.0 * row_count)[:, None]
    averaged_prediction = summed[0] / divisor
    averaged_observation = summed[1] / divisor
    prediction_mismatch = averaged_prediction - averaged_observation
    all_rows = jnp.arange(parallel_overall_accumulated, dtype=jnp.float32)
    cosine = jnp.cos(jnp.pi * (0.5 - all_rows / (parallel_overall_accumulated - 1)))
    weight_all = cosine / jnp.mean(cosine)
    cosine_factor_vector = lax.dynamic_slice_in_dim(
        weight_all, row_start, nearby_parallel_accumulated
    )[:, None]
    weighted_fcst = cosine_factor_vector * averaged_prediction
    weighted_true = cosine_factor_vector * averaged_observation
    running_accumulations = jnp.stack(
        [
            jnp.sum(cosine_factor_vector * prediction_mismatch * prediction_mismatch, axis=(1, 2)),
            jnp.sum(weighted_fcst, axis=(1, 2)),
            jnp.sum(weighted_true, axis=(1, 2)),
            jnp.sum(weighted_fcst * averaged_prediction, axis=(1, 2)),
            jnp.sum(weighted_true * averaged_observation, axis=(1, 2)),
            jnp.sum(weighted_fcst * averaged_observation, axis=(1, 2)),
        ]
    )
    totals = lax.psum(running_accumulations, ("lat", "lon"))
    quadratic_mean_mistake, pattern_agreement = finish(
        totals, float(parallel_overall_accumulated * meridian_accumulated)
    )
    return (prediction_mismatch.astype(jnp.bfloat16), quadratic_mean_mistake, pattern_agreement)


def solution(mesh):
    placed = (P(None, "lat", "lon"), P(None, "lat", "lon"), P(None, "lat", "lon"))
    return jax.shard_map(
        local,
        mesh=mesh,
        in_specs=placed,
        out_specs=(P(None, "lat", "lon"), P(), P()),
        check_vma=False,
    )
```

profile of v0, /device:TPU:0, one launch (start us, length us, event | category | flops | bytes accessed | tf_op | source)
XLA Modules:
  0.0 139.8 jit_solution(17298895487577244605)
XLA Ops:
  0.6 4.5 %copy.6 = bf16[222,40,128]{0,1,2:T(8,128)(2,1)S(1)} copy(bf16[222,40,128]{2,1,0:T(8,128)(2,1)} %param.3) | data formatting | bytes 4546560 | tf_op args[0]
  5.1 5.2 %copy.7 = bf16[222,40,128]{0,1,2:T(8,128)(2,1)} copy(bf16[222,40,128]{2,1,0:T(8,128)(2,1)} %param.4) | data formatting | bytes 4546560 | tf_op args[1]
  10.3 5.3 %copy.8 = bf16[222,40,128]{0,1,2:T(8,128)(2,1)} copy(bf16[222,40,128]{2,1,0:T(8,128)(2,1)} %param.5) | data formatting | bytes 4546560 | tf_op args[2]
  15.6 3.1 %pad_maximum_fusion.3 = (bf16[3,222,1,128]{1,2,3,0:T(2,128)(2,1)}, bf16[3,222,1,128]{1,2,3,0:T(2,128)(2,1)}) fusion(bf16[1,222,40,128]{1,2,3,0:T(8,128)(2,1)} %bitcast.25, bf16[1,222,40,128]{1,2,3,0:T(8,128)(2,1)} %bitcast.22, bf16[1,222,40,128]{1,2,3,0:T(8,128)(2,1)S(1)} %bitcast.19), kind=kLoop, calls=%fused_computation.30 | loop fusion | flops 1022976 | bytes 7160832 | tf_op jit(solution)/shard_map/slice | solution.py:13
  18.7 3.0 %collective-permute-start = (bf16[3,222,1,128]{1,2,3,0:T(2,128)(2,1)}, bf16[3,222,1,128]{1,2,3,0:T(2,128)(2,1)S(1)}, u32[]{:S(2)}, u32[]{:S(2)}) collective-permute-start(bf16[3,222,1,128]{1,2,3,0:T(2,128)(2,1)} %get-tuple-element.18), channel_id=1, source_target_pairs={{0,4},{4,8},{8,12},{12,16},{16,20},{20,24},{24,28},{28,0},{1,5},{5... | collective-permute-start | bytes 511496 | tf_op jit(solution)/shard_map/ppermute | solution.py:16
  21.7 3.0 %collective-permute-start.1 = (bf16[3,222,1,128]{1,2,3,0:T(2,128)(2,1)}, bf16[3,222,1,128]{1,2,3,0:T(2,128)(2,1)S(1)}, u32[]{:S(2)}, u32[]{:S(2)}) collective-permute-start(bf16[3,222,1,128]{1,2,3,0:T(2,128)(2,1)} %get-tuple-element.19), channel_id=1, source_target_pairs={{4,0},{8,4},{12,8},{16,12},{20,16},{24,20},{28,24},{0,28},{5,1},{9... | collective-permute-start | bytes 511496 | tf_op jit(solution)/shard_map/ppermute | solution.py:18
  24.8 0.7 fusion.11
  26.1 0.5 fusion.19
  26.6 0.6 fusion.10
  27.2 11.6 %collective-permute-done = bf16[3,222,1,128]{1,2,3,0:T(2,128)(2,1)S(1)} collective-permute-done((bf16[3,222,1,128]{1,2,3,0:T(2,128)(2,1)}, bf16[3,222,1,128]{1,2,3,0:T(2,128)(2,1)S(1)}, u32[]{:S(2)}, u32[]{:S(2)}) %collective-permute-start) | collective-permute-done | bytes 170528 | tf_op jit(solution)/shard_map/ppermute | solution.py:16
  38.8 2.1 %collective-permute-done.1 = bf16[3,222,1,128]{1,2,3,0:T(2,128)(2,1)S(1)} collective-permute-done((bf16[3,222,1,128]{1,2,3,0:T(2,128)(2,1)}, bf16[3,222,1,128]{1,2,3,0:T(2,128)(2,1)S(1)}, u32[]{:S(2)}, u32[]{:S(2)}) %collective-permute-start.1) | collective-permute-done | bytes 170528 | tf_op jit(solution)/shard_map/ppermute | solution.py:18
  40.9 1.5 %pad_maximum_fusion.8 = (bf16[3,222,42,1]{1,2,3,0:T(8,128)(2,1)}, bf16[3,222,42,1]{1,2,3,0:T(8,128)(2,1)}) fusion(bf16[3,222,1,128]{1,2,3,0:T(2,128)(2,1)S(1)} %collective-permute-done.1, bf16[3,222,1,128]{1,2,3,0:T(2,128)(2,1)S(1)} %collective-permute-done, bf16[1,222,40,128]{1,2,3,0:T(8,128)(2,1)} %bitcast.26, bf16[1,222,40,128]{1,2,3,0:T(8,128)(2,1)} %bitcast.23, ...), kind=kLoop, calls=%fused_computation.35 | loop fusion | flops 559440 | bytes 7272720 | tf_op jit(solution)/shard_map/slice | solution.py:13
  42.4 0.0 collective-permute-start.2
  42.4 1.7 %collective-permute-start.3 = (bf16[3,222,42,1]{1,2,3,0:T(8,128)(2,1)}, bf16[3,222,42,1]{1,2,3,0:T(8,128)(2,1)S(1)}, u32[]{:S(2)}, u32[]{:S(2)}) collective-permute-start(bf16[3,222,42,1]{1,2,3,0:T(8,128)(2,1)} %get-tuple-element.17), channel_id=1, source_target_pairs={{1,0},{2,1},{3,2},{0,3},{5,4},{6,5},{7,6},{4,7},{9,8},{10,9},{11,1... | collective-permute-start | bytes 167840 | tf_op jit(solution)/shard_map/ppermute | solution.py:18
  44.2 0.5 and_convert_fusion
  44.7 0.7 dynamic_slice.3
  45.4 0.0 copy-start.1
  45.4 1.0 collective-permute-done.2
  46.4 0.1 collective-permute-done.3
  46.5 10.1 %pad_maximum_fusion = bf16[3,222,42,130]{1,2,3,0:T(8,128)(2,1)S(1)} fusion(bf16[3,222,42,1]{1,2,3,0:T(8,128)(2,1)S(1)} %collective-permute-done.3, bf16[3,222,1,128]{1,2,3,0:T(2,128)(2,1)S(1)} %collective-permute-done.1, bf16[1,222,40,128]{1,2,3,0:T(8,128)(2,1)} %bitcast.27, bf16[1,222,40,128]{1,2,3,0:T(8,128)(2,1)} %bitcast.24, ...), kind=kLoop, calls=%fused_computation | loop fusion | flops 50909040 | bytes 14545440 | tf_op jit(solution)/shard_map/concatenate | solution.py:14
  56.6 0.0 copy-done.1
  56.6 5.5 %fusion.1 = (f32[222,42,130]{0,1,2:T(8,128)}, f32[222,42,130]{0,1,2:T(8,128)}) fusion(bf16[3,222,42,130]{1,2,3,0:T(8,128)(2,1)S(1)} %pad_maximum_fusion, f32[42]{0:T(128)S(1)} %copy-done.1), kind=kLoop, calls=%fused_computation.10 | loop fusion | flops 8484840 | bytes 16969848 | tf_op jit(solution)/shard_map/mul | solution.py:65
  62.1 0.0 copy-start
  62.1 16.3 %slice_add_fusion = (f32[222,40,130]{0,1,2:T(8,128)S(1)}, f32[222,40,130]{0,1,2:T(8,128)}) fusion(f32[222,42,130]{0,1,2:T(8,128)} %get-tuple-element.15, f32[222,42,130]{0,1,2:T(8,128)} %get-tuple-element.14), kind=kLoop, calls=%fused_computation.13 | loop fusion | flops 4617600 | bytes 36940800 | tf_op jit(solution)/shard_map/add | solution.py:34
  78.4 0.0 copy-done
  78.4 12.7 %fusion.5 = (f32[222]{0:T(256)S(1)}, f32[222]{0:T(256)S(1)}, f32[222]{0:T(256)S(1)}, f32[222]{0:T(256)S(1)}, f32[222]{0:T(256)S(1)}, /*index=5*/f32[222]{0:T(256...) fusion(f32[40]{0:T(128)S(1)} %dynamic_slice.3, f32[40]{0:T(128)S(1)} %copy-done, f32[222,40,130]{0,1,2:T(8,128)S(1)} %get-tuple-element.22, ...), kind=kLoop, calls=%fused_computation.18 | loop fusion | flops 22731468 | bytes 36378128 | tf_op jit(solution)/shard_map/reduce_sum | solution.py:90
  91.1 39.4 %psum.7 = f32[6,222]{1,0:T(8,128)S(1)} all-reduce(f32[6,222]{1,0:T(8,128)S(1)} %stack.43), channel_id=1, replica_groups=mesh['lat'=8,'lon'=4] {'lat','lon'}, use_global_device_ids=true, to_apply=%region_7.0 | all-reduce | flops 1332 | bytes 10656 | tf_op jit(solution)/shard_map/psum | solution.py:93
  130.5 0.6 fusion.15
  131.1 4.9 %subtract_convert_fusion = bf16[222,40,128]{0,1,2:T(8,128)(2,1)S(1)} fusion(f32[222,40,128]{0,1,2:T(8,128)} %get-tuple-element.13, f32[222,40,128]{0,1,2:T(8,128)} %get-tuple-element.12), kind=kLoop, calls=%fused_computation.27 | loop fusion | flops 2273280 | bytes 11366400 | tf_op jit(solution)/shard_map/convert_element_type | solution.py:97
  136.0 3.8 %copy.9 = bf16[222,40,128]{2,1,0:T(8,128)(2,1)} copy(bf16[222,40,128]{0,1,2:T(8,128)(2,1)S(1)} %subtract_convert_fusion) | data formatting | bytes 4546560
  (1 shorter events, 0.0 us)
Async XLA Ops:
  18.7 20.1 %collective-permute-start = (bf16[3,222,1,128]{1,2,3,0:T(2,128)(2,1)}, bf16[3,222,1,128]{1,2,3,0:T(2,128)(2,1)S(1)}, u32[]{:S(2)}, u32[]{:S(2)}) collective-permute-start(bf16[3,222,1,128]{1,2,3,0:T(2,128)(2,1)} %get-tuple-element.18), channel_id=1, source_target_pairs={{0,4},{4,8},{8,12},{12,16},{16,20},{20,24},{24,28},{28,0},{1,5},{5... | collective-permute-start | bytes 511496 | tf_op jit(solution)/shard_map/ppermute | solution.py:16
  21.7 19.2 %collective-permute-start.1 = (bf16[3,222,1,128]{1,2,3,0:T(2,128)(2,1)}, bf16[3,222,1,128]{1,2,3,0:T(2,128)(2,1)S(1)}, u32[]{:S(2)}, u32[]{:S(2)}) collective-permute-start(bf16[3,222,1,128]{1,2,3,0:T(2,128)(2,1)} %get-tuple-element.19), channel_id=1, source_target_pairs={{4,0},{8,4},{12,8},{16,12},{20,16},{24,20},{28,24},{0,28},{5,1},{9... | collective-permute-start | bytes 511496 | tf_op jit(solution)/shard_map/ppermute | solution.py:18
  42.4 4.0 %collective-permute-start.2 = (bf16[3,222,42,1]{1,2,3,0:T(8,128)(2,1)}, bf16[3,222,42,1]{1,2,3,0:T(8,128)(2,1)S(1)}, u32[]{:S(2)}, u32[]{:S(2)}) collective-permute-start(bf16[3,222,42,1]{1,2,3,0:T(8,128)(2,1)} %get-tuple-element.16), channel_id=1, source_target_pairs={{0,1},{1,2},{2,3},{3,0},{4,5},{5,6},{6,7},{7,4},{8,9},{9,10},{10,1... | collective-permute-start | bytes 167840 | tf_op jit(solution)/shard_map/ppermute | solution.py:16
  42.4 4.0 %collective-permute-start.3 = (bf16[3,222,42,1]{1,2,3,0:T(8,128)(2,1)}, bf16[3,222,42,1]{1,2,3,0:T(8,128)(2,1)S(1)}, u32[]{:S(2)}, u32[]{:S(2)}) collective-permute-start(bf16[3,222,42,1]{1,2,3,0:T(8,128)(2,1)} %get-tuple-element.17), channel_id=1, source_target_pairs={{1,0},{2,1},{3,2},{0,3},{5,4},{6,5},{7,6},{4,7},{9,8},{10,9},{11,1... | collective-permute-start | bytes 167840 | tf_op jit(solution)/shard_map/ppermute | solution.py:18
  45.4 11.1 %copy-start.1 = (f32[42]{0:T(128)S(1)}, f32[42]{0:T(128)}, u32[]{:S(2)}) copy-start(f32[42]{0:T(128)} %and_convert_fusion) | copy-start | bytes 508
  62.1 16.3 %copy-start = (f32[40]{0:T(128)S(1)}, f32[40]{0:T(128)}, u32[]{:S(2)}) copy-start(f32[40]{0:T(128)} %fusion.19) | copy-start | bytes 484
where the time goes:
time: 140 us
  other arithmetic  57 us (41%)
  blocking collectives  39.4 us (28%)
  local copies, waits for them, and re-layouts  19.5 us (14%)
  waiting for transfers between devices  14.7 us (10%)
  starting transfers between devices  7.78 us (6%)
    psum x1, blocking collectives, local(): totals = lax.psum(running_accumulations, ('lat', 'lon'))  39.4 us
    unnamed x8, local copies, waits for them, and re-layouts  18.7 us
    add x1, other arithmetic, vertical_sum(): return member[:, :-2] + member[:, 1:-1] + member[:, 2:]  16.3 us
    reduce_sum x1, other arithmetic, local(): jnp.sum(weighted_fcst * averaged_observation, axis=(1, 2))  12.7 us
    ppermute x2, waiting for transfers between devices, extended(): lax.ppermute(tail, axis, [(i, (i + 1) % count) for i in range(count)])  12.6 us
    concatenate x1, other arithmetic, extended(): jnp.concatenate([lax.ppermute(tail, axis, [(i, (i + 1) % count) for i in...  10.1 us
    mul x1, other arithmetic, local(): member * inside  5.51 us
    convert_element_type x1, other arithmetic, local(): prediction_mismatch.astype(jnp.bfloat16)  4.93 us
  transfers between devices with their start and end apart: 4, of which 4 were waited for; matrix products, arithmetic and copies ran while one was open for 2% of the time, Pallas kernels for 0%

commit v1 on v0

--- a/solution.py
+++ b/solution.py
@@ -90,7 +90,7 @@
             jnp.sum(weighted_fcst * averaged_observation, axis=(1, 2)),
         ]
     )
-    totals = lax.psum(running_accumulations, ("lat", "lon"))
+    totals = lax.psum(lax.psum(running_accumulations, "lon"), "lat")
     quadratic_mean_mistake, pattern_agreement = finish(
         totals, float(parallel_overall_accumulated * meridian_accumulated)
     )

time: 140 us -> 129 us (0.921)
  blocking collectives: 39.4 us -> 28.1 us
    psum x1 -> x2, blocking collectives: 39.4 us -> 28.1 us  [local(): totals = lax.psum(lax.psum(running_accumulations, 'lon'), 'lat')]
where the time goes in v1:
time: 129 us
  other arithmetic  57 us (44%)
  blocking collectives  28.1 us (22%)
  local copies, waits for them, and re-layouts  19.5 us (15%)
  waiting for transfers between devices  14.7 us (11%)
  starting transfers between devices  7.78 us (6%)
  between operations  1.34 us (1%)
    psum x2, blocking collectives, local(): totals = lax.psum(lax.psum(running_accumulations, 'lon'), 'lat')  28.1 us
    unnamed x8, local copies, waits for them, and re-layouts  18.7 us
    add x1, other arithmetic, vertical_sum(): return member[:, :-2] + member[:, 1:-1] + member[:, 2:]  16.3 us
    reduce_sum x1, other arithmetic, local(): jnp.sum(weighted_fcst * averaged_observation, axis=(1, 2))  12.7 us
    ppermute x2, waiting for transfers between devices, extended(): lax.ppermute(tail, axis, [(i, (i + 1) % count) for i in range(count)])  12.6 us
    concatenate x1, other arithmetic, extended(): jnp.concatenate([lax.ppermute(tail, axis, [(i, (i + 1) % count) for i in...  10.1 us
    mul x1, other arithmetic, local(): member * inside  5.51 us
    convert_element_type x1, other arithmetic, local(): prediction_mismatch.astype(jnp.bfloat16)  4.93 us
  transfers between devices with their start and end apart: 4, of which 4 were waited for; matrix products, arithmetic and copies ran while one was open for 2% of the time, Pallas kernels for 0%

profile of v1, /device:TPU:0, one launch (start us, length us, event | category | flops | bytes accessed | tf_op | source)
XLA Modules:
  0.0 128.5 jit_solution(118370961449659986)
XLA Ops:
  0.6 4.5 %copy.6 = bf16[222,40,128]{0,1,2:T(8,128)(2,1)S(1)} copy(bf16[222,40,128]{2,1,0:T(8,128)(2,1)} %param.3) | data formatting | bytes 4546560 | tf_op args[0]
  5.1 5.2 %copy.7 = bf16[222,40,128]{0,1,2:T(8,128)(2,1)} copy(bf16[222,40,128]{2,1,0:T(8,128)(2,1)} %param.4) | data formatting | bytes 4546560 | tf_op args[1]
  10.3 5.3 %copy.8 = bf16[222,40,128]{0,1,2:T(8,128)(2,1)} copy(bf16[222,40,128]{2,1,0:T(8,128)(2,1)} %param.5) | data formatting | bytes 4546560 | tf_op args[2]
  15.6 3.1 %pad_maximum_fusion.3 = (bf16[3,222,1,128]{1,2,3,0:T(2,128)(2,1)}, bf16[3,222,1,128]{1,2,3,0:T(2,128)(2,1)}) fusion(bf16[1,222,40,128]{1,2,3,0:T(8,128)(2,1)} %bitcast.25, bf16[1,222,40,128]{1,2,3,0:T(8,128)(2,1)} %bitcast.22, bf16[1,222,40,128]{1,2,3,0:T(8,128)(2,1)S(1)} %bitcast.19), kind=kLoop, calls=%fused_computation.30 | loop fusion | flops 1022976 | bytes 7160832 | tf_op jit(solution)/shard_map/slice | solution.py:13
  18.7 3.0 %collective-permute-start = (bf16[3,222,1,128]{1,2,3,0:T(2,128)(2,1)}, bf16[3,222,1,128]{1,2,3,0:T(2,128)(2,1)S(1)}, u32[]{:S(2)}, u32[]{:S(2)}) collective-permute-start(bf16[3,222,1,128]{1,2,3,0:T(2,128)(2,1)} %get-tuple-element.18), channel_id=1, source_target_pairs={{0,4},{4,8},{8,12},{12,16},{16,20},{20,24},{24,28},{28,0},{1,5},{5... | collective-permute-start | bytes 511496 | tf_op jit(solution)/shard_map/ppermute | solution.py:16
  21.7 3.0 %collective-permute-start.1 = (bf16[3,222,1,128]{1,2,3,0:T(2,128)(2,1)}, bf16[3,222,1,128]{1,2,3,0:T(2,128)(2,1)S(1)}, u32[]{:S(2)}, u32[]{:S(2)}) collective-permute-start(bf16[3,222,1,128]{1,2,3,0:T(2,128)(2,1)} %get-tuple-element.19), channel_id=1, source_target_pairs={{4,0},{8,4},{12,8},{16,12},{20,16},{24,20},{28,24},{0,28},{5,1},{9... | collective-permute-start | bytes 511496 | tf_op jit(solution)/shard_map/ppermute | solution.py:18
  24.8 0.7 fusion.11
  26.1 0.5 fusion.19
  26.6 0.6 fusion.10
  27.2 11.6 %collective-permute-done = bf16[3,222,1,128]{1,2,3,0:T(2,128)(2,1)S(1)} collective-permute-done((bf16[3,222,1,128]{1,2,3,0:T(2,128)(2,1)}, bf16[3,222,1,128]{1,2,3,0:T(2,128)(2,1)S(1)}, u32[]{:S(2)}, u32[]{:S(2)}) %collective-permute-start) | collective-permute-done | bytes 170528 | tf_op jit(solution)/shard_map/ppermute | solution.py:16
  38.8 2.1 %collective-permute-done.1 = bf16[3,222,1,128]{1,2,3,0:T(2,128)(2,1)S(1)} collective-permute-done((bf16[3,222,1,128]{1,2,3,0:T(2,128)(2,1)}, bf16[3,222,1,128]{1,2,3,0:T(2,128)(2,1)S(1)}, u32[]{:S(2)}, u32[]{:S(2)}) %collective-permute-start.1) | collective-permute-done | bytes 170528 | tf_op jit(solution)/shard_map/ppermute | solution.py:18
  40.9 1.5 %pad_maximum_fusion.8 = (bf16[3,222,42,1]{1,2,3,0:T(8,128)(2,1)}, bf16[3,222,42,1]{1,2,3,0:T(8,128)(2,1)}) fusion(bf16[3,222,1,128]{1,2,3,0:T(2,128)(2,1)S(1)} %collective-permute-done.1, bf16[3,222,1,128]{1,2,3,0:T(2,128)(2,1)S(1)} %collective-permute-done, bf16[1,222,40,128]{1,2,3,0:T(8,128)(2,1)} %bitcast.26, bf16[1,222,40,128]{1,2,3,0:T(8,128)(2,1)} %bitcast.23, ...), kind=kLoop, calls=%fused_computation.35 | loop fusion | flops 559440 | bytes 7272720 | tf_op jit(solution)/shard_map/slice | solution.py:13
  42.4 0.0 collective-permute-start.2
  42.4 1.7 %collective-permute-start.3 = (bf16[3,222,42,1]{1,2,3,0:T(8,128)(2,1)}, bf16[3,222,42,1]{1,2,3,0:T(8,128)(2,1)S(1)}, u32[]{:S(2)}, u32[]{:S(2)}) collective-permute-start(bf16[3,222,42,1]{1,2,3,0:T(8,128)(2,1)} %get-tuple-element.17), channel_id=1, source_target_pairs={{1,0},{2,1},{3,2},{0,3},{5,4},{6,5},{7,6},{4,7},{9,8},{10,9},{11,1... | collective-permute-start | bytes 167840 | tf_op jit(solution)/shard_map/ppermute | solution.py:18
  44.2 0.5 and_convert_fusion
  44.7 0.7 dynamic_slice.3
  45.4 0.0 copy-start.1
  45.4 1.0 collective-permute-done.2
  46.4 0.1 collective-permute-done.3
  46.5 10.1 %pad_maximum_fusion = bf16[3,222,42,130]{1,2,3,0:T(8,128)(2,1)S(1)} fusion(bf16[3,222,42,1]{1,2,3,0:T(8,128)(2,1)S(1)} %collective-permute-done.3, bf16[3,222,1,128]{1,2,3,0:T(2,128)(2,1)S(1)} %collective-permute-done.1, bf16[1,222,40,128]{1,2,3,0:T(8,128)(2,1)} %bitcast.27, bf16[1,222,40,128]{1,2,3,0:T(8,128)(2,1)} %bitcast.24, ...), kind=kLoop, calls=%fused_computation | loop fusion | flops 50909040 | bytes 14545440 | tf_op jit(solution)/shard_map/concatenate | solution.py:14
  56.6 0.0 copy-done.1
  56.6 5.5 %fusion.1 = (f32[222,42,130]{0,1,2:T(8,128)}, f32[222,42,130]{0,1,2:T(8,128)}) fusion(bf16[3,222,42,130]{1,2,3,0:T(8,128)(2,1)S(1)} %pad_maximum_fusion, f32[42]{0:T(128)S(1)} %copy-done.1), kind=kLoop, calls=%fused_computation.10 | loop fusion | flops 8484840 | bytes 16969848 | tf_op jit(solution)/shard_map/mul | solution.py:65
  62.1 0.0 copy-start
  62.1 16.3 %slice_add_fusion = (f32[222,40,130]{0,1,2:T(8,128)S(1)}, f32[222,40,130]{0,1,2:T(8,128)}) fusion(f32[222,42,130]{0,1,2:T(8,128)} %get-tuple-element.15, f32[222,42,130]{0,1,2:T(8,128)} %get-tuple-element.14), kind=kLoop, calls=%fused_computation.13 | loop fusion | flops 4617600 | bytes 36940800 | tf_op jit(solution)/shard_map/add | solution.py:34
  78.4 0.0 copy-done
  78.4 12.7 %fusion.5 = (f32[222]{0:T(256)S(1)}, f32[222]{0:T(256)S(1)}, f32[222]{0:T(256)S(1)}, f32[222]{0:T(256)S(1)}, f32[222]{0:T(256)S(1)}, /*index=5*/f32[222]{0:T(256...) fusion(f32[40]{0:T(128)S(1)} %dynamic_slice.3, f32[40]{0:T(128)S(1)} %copy-done, f32[222,40,130]{0,1,2:T(8,128)S(1)} %get-tuple-element.22, ...), kind=kLoop, calls=%fused_computation.18 | loop fusion | flops 22731468 | bytes 36378128 | tf_op jit(solution)/shard_map/reduce_sum | solution.py:90
  91.1 7.4 %psum.14 = f32[6,222]{1,0:T(8,128)S(1)} all-reduce(f32[6,222]{1,0:T(8,128)S(1)} %stack.43), channel_id=1, replica_groups=mesh['lat'=8,'lon'=4] {'lon'}, use_global_device_ids=true, to_apply=%region_7.0 | all-reduce | flops 1332 | bytes 10656 | tf_op jit(solution)/shard_map/psum | solution.py:93
  98.5 20.7 %psum.15 = f32[6,222]{1,0:T(8,128)S(1)} all-reduce(f32[6,222]{1,0:T(8,128)S(1)} %psum.14), channel_id=1, replica_groups=mesh['lat'=8,'lon'=4] {'lat'}, use_global_device_ids=true, to_apply=%region_8.0 | all-reduce | flops 1332 | bytes 10656 | tf_op jit(solution)/shard_map/psum | solution.py:93
  119.2 0.6 fusion.15
  119.8 4.9 %subtract_convert_fusion = bf16[222,40,128]{0,1,2:T(8,128)(2,1)S(1)} fusion(f32[222,40,128]{0,1,2:T(8,128)} %get-tuple-element.13, f32[222,40,128]{0,1,2:T(8,128)} %get-tuple-element.12), kind=kLoop, calls=%fused_computation.27 | loop fusion | flops 2273280 | bytes 11366400 | tf_op jit(solution)/shard_map/convert_element_type | solution.py:97
  124.8 3.8 %copy.9 = bf16[222,40,128]{2,1,0:T(8,128)(2,1)} copy(bf16[222,40,128]{0,1,2:T(8,128)(2,1)S(1)} %subtract_convert_fusion) | data formatting | bytes 4546560
  (1 shorter events, 0.0 us)
Async XLA Ops:
  18.7 20.1 %collective-permute-start = (bf16[3,222,1,128]{1,2,3,0:T(2,128)(2,1)}, bf16[3,222,1,128]{1,2,3,0:T(2,128)(2,1)S(1)}, u32[]{:S(2)}, u32[]{:S(2)}) collective-permute-start(bf16[3,222,1,128]{1,2,3,0:T(2,128)(2,1)} %get-tuple-element.18), channel_id=1, source_target_pairs={{0,4},{4,8},{8,12},{12,16},{16,20},{20,24},{24,28},{28,0},{1,5},{5... | collective-permute-start | bytes 511496 | tf_op jit(solution)/shard_map/ppermute | solution.py:16
  21.7 19.2 %collective-permute-start.1 = (bf16[3,222,1,128]{1,2,3,0:T(2,128)(2,1)}, bf16[3,222,1,128]{1,2,3,0:T(2,128)(2,1)S(1)}, u32[]{:S(2)}, u32[]{:S(2)}) collective-permute-start(bf16[3,222,1,128]{1,2,3,0:T(2,128)(2,1)} %get-tuple-element.19), channel_id=1, source_target_pairs={{4,0},{8,4},{12,8},{16,12},{20,16},{24,20},{28,24},{0,28},{5,1},{9... | collective-permute-start | bytes 511496 | tf_op jit(solution)/shard_map/ppermute | solution.py:18
  42.4 4.0 %collective-permute-start.2 = (bf16[3,222,42,1]{1,2,3,0:T(8,128)(2,1)}, bf16[3,222,42,1]{1,2,3,0:T(8,128)(2,1)S(1)}, u32[]{:S(2)}, u32[]{:S(2)}) collective-permute-start(bf16[3,222,42,1]{1,2,3,0:T(8,128)(2,1)} %get-tuple-element.16), channel_id=1, source_target_pairs={{0,1},{1,2},{2,3},{3,0},{4,5},{5,6},{6,7},{7,4},{8,9},{9,10},{10,1... | collective-permute-start | bytes 167840 | tf_op jit(solution)/shard_map/ppermute | solution.py:16
  42.4 4.0 %collective-permute-start.3 = (bf16[3,222,42,1]{1,2,3,0:T(8,128)(2,1)}, bf16[3,222,42,1]{1,2,3,0:T(8,128)(2,1)S(1)}, u32[]{:S(2)}, u32[]{:S(2)}) collective-permute-start(bf16[3,222,42,1]{1,2,3,0:T(8,128)(2,1)} %get-tuple-element.17), channel_id=1, source_target_pairs={{1,0},{2,1},{3,2},{0,3},{5,4},{6,5},{7,6},{4,7},{9,8},{10,9},{11,1... | collective-permute-start | bytes 167840 | tf_op jit(solution)/shard_map/ppermute | solution.py:18
  45.4 11.1 %copy-start.1 = (f32[42]{0:T(128)S(1)}, f32[42]{0:T(128)}, u32[]{:S(2)}) copy-start(f32[42]{0:T(128)} %and_convert_fusion) | copy-start | bytes 508
  62.1 16.3 %copy-start = (f32[40]{0:T(128)S(1)}, f32[40]{0:T(128)}, u32[]{:S(2)}) copy-start(f32[40]{0:T(128)} %fusion.19) | copy-start | bytes 484
